TPU v7x, 128 devices: a whole 4x4x4 slice. The times are simulated.
128 devices in a mesh: node: 32 (over x, z, core), dev: 4 (over y).
Axes of the slice: x: 4, y: 4, z: 4, core: 2. Of those that a mesh axis runs over, the one named last changes fastest.
Arguments:
- kv_pages: bfloat16 [16384, 1, 2, 16, 1024], P(('node', 'dev')), may hold values from -6 to 6
- new_slot: int32 [16384], P(('node', 'dev')), may hold values from 0 to 16383, as said below
- request_rate: float32 [2048], P(('node', 'dev')), may hold values from 0.25 to 4
- page_table: int32 [2048, 128], P(('node', 'dev')), may hold values from 0 to 16383
Outputs:
- migrated: bfloat16 [16384, 1, 2, 16, 1024], P(('node', 'dev'))
- device_load: float32 [128], replicated
Inputs may be any that keep to these rules, and one draw needn't show every extreme that they name: new_slot is a permutation of the slots; slot p lies on device p // 128. Every device sends exactly 127 of its pages to other devices, at most one to any one device, and receives exactly 127 into the slots that its leaving pages free; its other pages keep their slots.
All inputs are finite; a program needn't handle non-finite values.
Results may differ from a plain program's by a relative error of at most 0.001.
Values may be sent and summed in bfloat16 or wider, within the bound.
A program may use at most 128 MiB of HBM per device.

v0:
```python
import functools

import jax
import jax.numpy as jnp
from jax import lax
from jax.sharding import Mesh
from jax.sharding import PartitionSpec as P

NODE_DEV = ("node_0", "node_1", "node_2", "dev")


def sum_in_order(tiles, axes, sequence):
    shape = [lax.axis_size(a) for a in axes]
    tiles = tiles.reshape(*shape, *tiles.shape[1:])
    tiles = tiles.transpose(*sequence, *range(len(axes), tiles.ndim))
    tiles = tiles.reshape(-1, *tiles.shape[len(axes) :])
    for k in sequence:
        tiles = lax.psum_scatter(tiles, axes[k], scatter_dimension=0, tiled=True)
    return tiles[0]


def in_blocks(value, dim, devices):
    before, after = (value.shape[:dim], value.shape[dim + 1 :])
    return jnp.moveaxis(value.reshape(*before, devices, -1, *after), dim, 0)


def sum_by_axis(value, axes, sequence, dim):
    devices = lax.axis_size(axes)
    return sum_in_order(in_blocks(value, dim, devices), axes, sequence)


def by_axis(value, axes):
    return functools.reduce(lax.psum, axes, value)


def on_device(kv_pages, new_slot, request_rate, page_table):
    page_dev = kv_pages.shape[0]
    devices = lax.axis_size(NODE_DEV)
    myself = lax.axis_index(NODE_DEV)
    owners = new_slot // page_dev
    local_ids = jnp.arange(page_dev, dtype=jnp.int32)
    targets = jnp.arange(devices, dtype=jnp.int32)
    flat_pages = kv_pages.reshape(page_dev, -1)
    leaving = owners != myself
    matches = owners[:, None] == targets[None, :]
    sending = jnp.logical_and(matches, leaving[:, None])
    pack_sel = sending.T.astype(jnp.bfloat16)
    outgoing = jnp.dot(pack_sel, flat_pages, preferred_element_type=jnp.float32).astype(
        jnp.bfloat16
    )
    outgoing = outgoing.reshape((devices,) + kv_pages.shape[1:])
    local_target = new_slot % page_dev
    dest_local = jnp.sum(jnp.where(sending, local_target[:, None], 0), axis=0)
    filled = jnp.any(sending, axis=0)
    dest_local = jnp.where(filled, dest_local, page_dev)
    arrived, arrived_slot = (
        lax.all_to_all(outgoing, NODE_DEV, split_axis=0, concat_axis=0, tiled=True),
        lax.all_to_all(dest_local, NODE_DEV, split_axis=0, concat_axis=0, tiled=True),
    )
    weights = jnp.broadcast_to(request_rate[:, None], page_table.shape).reshape(-1)
    heat_local = (
        jnp.zeros((devices * page_dev,), jnp.float32).at[page_table.reshape(-1)].add(weights)
    )
    heat_own = sum_by_axis(heat_local, NODE_DEV, (2, 0, 1, 3), 0)
    owner_terms = jnp.sum(jnp.where(matches, heat_own[:, None], 0.0), axis=0)
    summed = by_axis(owner_terms, NODE_DEV)
    device_load = summed / (page_table.shape[1] * page_table.shape[0])
    place_hit = arrived_slot[None, :] == local_ids[:, None]
    place_sel = place_hit.astype(jnp.bfloat16)
    received = jnp.dot(
        place_sel, arrived.reshape(devices, -1), preferred_element_type=jnp.float32
    ).astype(jnp.bfloat16)
    arrival = jnp.any(place_hit, axis=1)
    migrated = jnp.where(arrival[:, None], received, flat_pages).reshape(kv_pages.shape)
    return (migrated, device_load)


def solution(mesh):
    split = Mesh(
        mesh.devices.reshape(4, 4, 2, mesh.shape["dev"]), ("node_0", "node_1", "node_2", "dev")
    )
    placed = (P(NODE_DEV, None, None, None, None), P(NODE_DEV), P(NODE_DEV), P(NODE_DEV, None))
    return jax.shard_map(
        on_device,
        mesh=split,
        in_specs=placed,
        out_specs=(P(NODE_DEV, None, None, None, None), P()),
        check_vma=False,
    )
```

profile of v0, /device:TPU:1, one launch (start us, length us, event | category | flops | bytes accessed | tf_op | source)
XLA Modules:
  0.0 246.4 jit_solution(339036951806925138)
XLA Ops:
  7.2 0.0 copy-start
  7.2 0.7 and_select_fusion
  7.9 0.7 broadcast_compare_fusion
  8.5 0.1 fusion.4
  8.6 0.1 select_reduce_fusion.1
  8.8 0.7 copy.18
  9.5 11.5 %all-to-all-start = ((s32[128,1,1]{2,1,0:T(1,128)}), s32[128,1,1]{2,1,0:T(1,128)S(1)}, u32[]{:S(2)}, u32[]{:S(2)}) async-start(s32[128,1,1]{2,1,0:T(1,128)} %copy.18), calls=%async_computation | async-start | bytes 131072 | tf_op jit(solution)/shard_map/all_to_all | solution.py:58
  21.0 12.8 %copy.22 = bf16[16,8,32,1024]{3,1,2,0:T(8,128)(2,1)} copy(bf16[16,8,32,1024]{3,2,1,0:T(8,128)(2,1)} %bitcast.40) | data formatting | bytes 16777216
  33.8 9.0 %convolution_convert_fusion.1 = bf16[128,32768]{1,0:T(8,128)(2,1)} fusion(bf16[128,32768]{1,0:T(8,128)(2,1)} %bitcast.34, s32[128]{0:T(128)S(1)} %get-tuple-element.15, pred[128]{0:T(512)(128)(4,1)S(1)} %get-tuple-element.14), kind=kOutput, calls=%fused_computation.2 | convolution fusion | flops 1077968896 | bytes 16777856 | tf_op jit(solution)/shard_map/dot_general | solution.py:48
  42.9 12.4 %copy.23 = bf16[16,8,32,1024]{3,2,1,0:T(8,128)(2,1)} copy(bf16[16,8,32,1024]{3,1,2,0:T(8,128)(2,1)} %bitcast.39) | data formatting | bytes 16777216
  55.3 0.0 all-to-all-done
  55.3 0.0 copy-start.1
  55.3 0.0 copy-start.3
  55.3 0.0 copy-start.2
  55.3 10.2 %all-to-all-start.1 = ((bf16[128,1,2,16,1024]{4,3,2,1,0:T(8,128)(2,1)}), bf16[128,1,2,16,1024]{4,3,2,1,0:T(8,128)(2,1)}, u32[]{:S(2)}, u32[]{:S(2)}) async-start(bf16[128,1,2,16,1024]{4,3,2,1,0:T(8,128)(2,1)} %bitcast.36), calls=%async_computation.1 | async-start | bytes 16777216 | tf_op jit(solution)/shard_map/all_to_all | solution.py:57
  65.5 0.0 reduce-scatter.3.cloned.1.call-start
  65.6 0.0 copy-done
  65.6 0.1 broadcast_bitcast_fusion
  65.6 0.0 copy-done.1
  65.7 11.3 %scatter_custom_fusion = f32[16384]{0:T(1024)S(1)} fusion(s32[2048]{0:T(1024)S(1)} %bitcast.45, f32[2048]{0:T(1024)S(1)} %broadcast_bitcast_fusion, f32[]{:T(128)} %constant.59.clone.1), kind=kCustom, calls=%fused_computation.12 | custom fusion | flops 2048 | bytes 65540 | tf_op jit(solution)/shard_map/scatter-add | solution.py:62
  76.9 0.6 copy.20
  77.6 0.0 reduce-scatter.3.cloned.1.call-update
  77.6 0.0 reduce-scatter.5.cloned.1.call-start
  77.6 0.0 copy-done.3
  77.7 0.6 dynamic-slice
  78.2 0.0 copy-done.2
  78.2 0.7 dynamic-slice.2
  79.6 2.4 reduce
  81.9 8.0 %reduce-scatter.3.cloned.1.call-done = f32[64,128]{1,0:T(8,128)} async-done(((f32[128,128]{1,0:T(8,128)}), f32[64,128]{1,0:T(8,128)}) %reduce-scatter.3.cloned.1.call-update) | async-done | bytes 32784 | tf_op jit(solution)/shard_map/reduce_scatter | solution.py:18
  89.9 0.0 reduce-scatter.5.cloned.1.call-update
  89.9 0.1 fusion.1
  90.0 24.3 %reduce-scatter.5.cloned.1.call-done = f32[16,128]{1,0:T(8,128)} async-done(((f32[64,128]{1,0:T(8,128)}), f32[16,128]{1,0:T(8,128)}) %reduce-scatter.5.cloned.1.call-update) | async-done | bytes 8208 | tf_op jit(solution)/shard_map/reduce_scatter | solution.py:18
  114.3 19.4 %all-reduce = f32[16,128]{1,0:T(8,128)S(1)} all-reduce(f32[16,128]{1,0:T(8,128)} %reduce-scatter.5.cloned.1.call-done), channel_id=4, replica_groups=mesh['node_0'=4,'node_1'=4,'node_2'=2,'dev'=4] {'node_1'}, use_global_device_ids=true, to_apply=%region_6.7.clone | all-reduce | flops 2048 | bytes 16384
  133.7 32.9 %all-reduce.1 = f32[4,128]{1,0:T(4,128)S(1)} all-reduce(f32[4,128]{1,0:T(4,128)S(1)} %constant_dynamic-slice_fusion.1), channel_id=5, replica_groups=mesh['node_0'=4,'node_1'=4,'node_2'=2,'dev'=4] {'dev'}, use_global_device_ids=true, to_apply=%region_7.8.clone | all-reduce | flops 512 | bytes 4096
  166.6 0.7 fusion.10
  167.3 0.1 select_reduce_fusion
  167.4 7.9 %psum.28 = f32[128]{0:T(128)S(1)} all-reduce(f32[128]{0:T(128)S(1)} %select_reduce_fusion), channel_id=1, replica_groups=mesh['node_0'=4,'node_1'=4,'node_2'=2,'dev'=4] {'node_0'}, use_global_device_ids=true, to_apply=%region_9.10 | all-reduce | flops 128 | bytes 1024 | tf_op jit(solution)/shard_map/psum | solution.py:33
  175.3 11.5 %psum.29 = f32[128]{0:T(128)S(1)} all-reduce(f32[128]{0:T(128)S(1)} %psum.28), channel_id=1, replica_groups=mesh['node_0'=4,'node_1'=4,'node_2'=2,'dev'=4] {'node_1'}, use_global_device_ids=true, to_apply=%region_10.11 | all-reduce | flops 128 | bytes 1024 | tf_op jit(solution)/shard_map/psum | solution.py:33
  186.8 9.3 %psum.30 = f32[128]{0:T(128)S(1)} all-reduce(f32[128]{0:T(128)S(1)} %psum.29), channel_id=1, replica_groups=mesh['node_0'=4,'node_1'=4,'node_2'=2,'dev'=4] {'node_2'}, use_global_device_ids=true, to_apply=%region_11.12 | all-reduce | flops 128 | bytes 1024 | tf_op jit(solution)/shard_map/psum | solution.py:33
  196.1 6.6 %psum.31 = f32[128]{0:T(128)S(1)} all-reduce(f32[128]{0:T(128)S(1)} %psum.30), channel_id=1, replica_groups=mesh['node_0'=4,'node_1'=4,'node_2'=2,'dev'=4] {'dev'}, use_global_device_ids=true, to_apply=%region_12.13 | all-reduce | flops 128 | bytes 1024 | tf_op jit(solution)/shard_map/psum | solution.py:33
  202.7 0.5 broadcast_multiply_fusion
  203.2 0.0 all-to-all-done.1
  203.2 12.6 %copy.24 = bf16[16,8,32,1024]{3,1,2,0:T(8,128)(2,1)} copy(bf16[16,8,32,1024]{3,2,1,0:T(8,128)(2,1)} %bitcast.21) | data formatting | bytes 16777216
  215.8 11.3 %fusion = bf16[128,32768]{1,0:T(8,128)(2,1)} fusion(bf16[128,32768]{1,0:T(8,128)(2,1)} %bitcast.35, bf16[128,32768]{1,0:T(8,128)(2,1)} %bitcast.37, pred[128]{0:T(512)(128)(4,1)S(1)} %fusion.1, s32[128]{0:T(128)S(1)} %reduce), kind=kOutput, calls=%fused_computation.3 | convolution fusion | flops 1082146816 | bytes 25166464 | tf_op jit(solution)/shard_map/dot_general | solution.py:70
  227.1 12.4 %copy.25 = bf16[16,8,32,1024]{3,2,1,0:T(8,128)(2,1)} copy(bf16[16,8,32,1024]{3,1,2,0:T(8,128)(2,1)} %bitcast.38) | data formatting | bytes 16777216
  (3 shorter events, 0.0 us)
Async XLA Ops:
  7.2 58.4 %copy-start = (f32[16]{0:T(128)S(1)}, f32[16]{0:T(128)}, u32[]{:S(2)}) copy-start(f32[16]{0:T(128)} %param.6) | copy-start | bytes 196
  9.5 45.7 %all-to-all-start = ((s32[128,1,1]{2,1,0:T(1,128)}), s32[128,1,1]{2,1,0:T(1,128)S(1)}, u32[]{:S(2)}, u32[]{:S(2)}) async-start(s32[128,1,1]{2,1,0:T(1,128)} %copy.18), calls=%async_computation | async-start | bytes 131072 | tf_op jit(solution)/shard_map/all_to_all | solution.py:58
  55.3 10.4 %copy-start.1 = (s32[16,128]{1,0:T(8,128)S(1)}, s32[16,128]{1,0:T(8,128)}, u32[]{:S(2)}) copy-start(s32[16,128]{1,0:T(8,128)} %param.7) | copy-start | bytes 24580
  55.3 22.4 %copy-start.3 = (u32[128]{0:T(128)S(1)}, u32[128]{0:T(128)}, u32[]{:S(2)}) copy-start(u32[128]{0:T(128)} %constant.66) | copy-start | bytes 1540
  55.3 23.0 %copy-start.2 = (u32[128]{0:T(128)S(1)}, u32[128]{0:T(128)}, u32[]{:S(2)}) copy-start(u32[128]{0:T(128)} %constant.70) | copy-start | bytes 1540
  55.3 147.9 %all-to-all-start.1 = ((bf16[128,1,2,16,1024]{4,3,2,1,0:T(8,128)(2,1)}), bf16[128,1,2,16,1024]{4,3,2,1,0:T(8,128)(2,1)}, u32[]{:S(2)}, u32[]{:S(2)}) async-start(bf16[128,1,2,16,1024]{4,3,2,1,0:T(8,128)(2,1)} %bitcast.36), calls=%async_computation.1 | async-start | bytes 16777216 | tf_op jit(solution)/shard_map/all_to_all | solution.py:57
  65.5 24.4 %reduce-scatter.3.cloned.1.call-start = ((), (), s32[]{:S(2)}) async-start(), calls=%async_computation.4 | async-start | bytes 98304 | tf_op jit(solution)/shard_map/reduce_scatter | solution.py:18
  77.6 36.7 %reduce-scatter.5.cloned.1.call-start = ((), (), s32[]{:S(2)}) async-start(), calls=%async_computation.5 | async-start | bytes 40960 | tf_op jit(solution)/shard_map/reduce_scatter | solution.py:18
Sparse Core Ops, SparseCore 0:
  77.7 12.1 reduce-scatter.2
  92.2 22.0 reduce-scatter.4
where the time goes:
time: 248 us; the launch traced here: 246 us
  blocking collectives  87.5 us (35%)
  local copies, waits for them, and re-layouts  53.6 us (22%)
  waiting for transfers between devices  32.3 us (13%)
  starting transfers between devices  21.8 us (9%)
  matrix products  20.3 us (8%)
  other arithmetic  16 us (6%)
  between operations  14.8 us (6%)
    unnamed x2, blocking collectives  52.3 us
    unnamed x15, local copies, waits for them, and re-layouts  51.5 us
    psum x4, blocking collectives, by_axis(): return functools.reduce(lax.psum, axes, value)  35.3 us
    reduce_scatter x2, waiting for transfers between devices, sum_in_order(): tiles = lax.psum_scatter(tiles, axes[k], scatter_dimension=0, tiled=True)  32.3 us
    all_to_all x1, starting transfers between devices, on_device(): lax.all_to_all(dest_local, NODE_DEV, split_axis=0, concat_axis=0, tiled=T...  11.5 us
    dot_general x1, matrix products, on_device(): jnp.dot(place_sel, arrived.reshape(devices, -1), preferred_element_type=j...  11.3 us
    scatter-add x1, other arithmetic, on_device(): jnp.zeros((devices * page_dev,), jnp.float32).at[page_table.reshape(-1)]  11.3 us
    all_to_all x1, starting transfers between devices, on_device(): lax.all_to_all(outgoing, NODE_DEV, split_axis=0, concat_axis=0, tiled=True)  10.2 us
  transfers between devices with their start and end apart: 4, of which 2 were waited for; matrix products, arithmetic and copies ran while one was open for 21% of the time, Pallas kernels for 0%

commit v1 on v0

v1 whole, which is shorter than its diff:
```python
import jax
import jax.numpy as jnp
import numpy as np
from jax import lax
from jax.experimental import pallas as pl
from jax.experimental.pallas import tpu as pltpu
from jax.sharding import Mesh
from jax.sharding import PartitionSpec as P

AXES = ("x", "z", "c", "y")
SIZE = {"x": 4, "z": 4, "c": 2, "y": 4}
DEVICES = 128
ORDERS = (("x", "y", "z"), ("y", "z", "x"), ("z", "x", "y"))
LATE = (2, 1, 3, 0)
AWAY = (2, 1, 3)


def make_plan():
    keyed = []
    for rel in range(DEVICES):
        step = {"x": rel // 32, "z": rel // 8 % 4, "c": rel // 4 % 2, "y": rel % 4}
        group = sum(step.values()) % 3
        first, second, third = (step[a] for a in ORDERS[group])
        keyed.append((group, first, second, third, step["c"], rel))
    keyed.sort()
    place = np.zeros((DEVICES,), np.int32)
    chunks = {}
    for row, (group, first, second, third, core, rel) in enumerate(keyed):
        place[rel] = row
        chunks.setdefault((group, first, second), []).append((row, third, core))
    return place, chunks


PLACE, CHUNKS = make_plan()


def my_index():
    at = [lax.axis_index(a) for a in AXES]
    return ((at[0] * 4 + at[1]) * 2 + at[2]) * 4 + at[3]


def partner(**steps):
    return tuple(
        jnp.bitwise_xor(lax.axis_index(a), steps[a]) if steps.get(a) else lax.axis_index(a)
        for a in AXES
    )


def along(axis, step, core=0):
    return partner(**{axis: step, "c": core})


def pack_kernel(slot_ref, place_ref, pages_ref, out_ref, sem):
    me = my_index()

    @pl.loop(0, DEVICES)
    def _(p):
        row = place_ref[jnp.bitwise_xor(lax.shift_right_logical(slot_ref[p], 7), me)]
        pltpu.make_async_copy(pages_ref.at[p, 0], out_ref.at[row], sem).start()

    pltpu.make_async_copy(out_ref, out_ref, sem).wait()


def place_kernel(slot_ref, place_ref, total_ref, pages_ref, out_ref, load_ref, sem):
    me = my_index()

    @pl.loop(0, DEVICES)
    def _(e):
        row = place_ref[jnp.bitwise_xor(e, me)]
        pltpu.make_async_copy(pages_ref.at[row], out_ref.at[slot_ref[0, e], 0], sem).start()

    load_ref[...] = total_ref[...] * (1.0 / 2048.0)
    pltpu.make_async_copy(pages_ref, pages_ref, sem).wait()


def exchange_kernel(
    rate_ref, table_ref, slots_ref, send_ref,
    pages_ref, slot_out_ref, load_ref,
    mid1, mid2, known, row1, row2, row3, part1, part2, part3,
    sent, got1, got2, got3, local, small_sent, small_got,
):
    x, z, c, y = (lax.axis_index(a) for a in AXES)
    me = my_index()
    row = c * 4 + y
    remote = lambda src, dst, ss, rs, dev: pltpu.make_async_remote_copy(
        src, dst, ss, rs, device_id=dev, device_id_type=pl.DeviceIdType.MESH
    )

    def wait(ref, sem):
        pltpu.make_async_copy(ref, ref, sem).wait()

    keep = pltpu.make_async_copy(slots_ref, known.at[x, z, pl.ds(row, 1)], local.at[0])
    keep.start()
    barrier = pltpu.get_barrier_semaphore()
    peers = [partner(c=1)] + [along(a, s, k) for a in "xyz" for s in AWAY for k in (0, 1)]
    for dev in peers:
        pl.semaphore_signal(barrier, inc=1, device_id=dev, device_id_type=pl.DeviceIdType.MESH)
    pl.semaphore_wait(barrier, len(peers))

    cell = [partner(c=k, y=s) for k in (0, 1) for s in range(4) if k or s]

    def span(key):
        rows = CHUNKS[key]
        return pl.ds(rows[0][0], len(rows))

    def spot(key):
        return (key[0] * 4 + key[1]) * 4 + key[2]

    def source(key):
        return mid2 if key[2] else (mid1 if key[1] else send_ref)

    def phase1(key):
        remote(
            send_ref.at[span(key)], mid1.at[span(key)], sent.at[0], got1.at[spot(key)],
            along(ORDERS[key[0]][0], key[1]),
        ).start()

    def phase2(key):
        src = mid1 if key[1] else send_ref
        remote(
            src.at[span(key)], mid2.at[span(key)], sent.at[1], got2.at[spot(key)],
            along(ORDERS[key[0]][1], key[2]),
        ).start()

    def phase3(key):
        src = source(key)
        for page, step, core in CHUNKS[key]:
            if step or core:
                remote(
                    src.at[page], pages_ref.at[page], sent.at[2], got3,
                    along(ORDERS[key[0]][2], step, core),
                ).start()
            else:
                pltpu.make_async_copy(src.at[page], pages_ref.at[page], local.at[1]).start()

    def start1(second):
        for first in AWAY:
            for g in range(3):
                phase1((g, first, second))

    def forward2(second):
        for first in AWAY:
            for g in range(3):
                key = (g, first, second)
                wait(mid1.at[span(key)], got1.at[spot(key)])
                phase2(key)

    def tell(src, dst, k, devs):
        for dev in devs:
            remote(src, dst, small_sent.at[k], small_got.at[k], dev).start()

    zs = [partner(z=s) for s in AWAY]
    xs = [partner(x=s) for s in AWAY]

    tell(slots_ref, known.at[x, z, pl.ds(row, 1)], 0, cell)
    start1(2)
    keep.wait()
    wait(known.at[0, 0, pl.ds(0, 7)], small_got.at[0])
    tell(known.at[x, z], known.at[x, z], 1, zs)
    start1(1)
    wait(known.at[0, pl.ds(0, 3)], small_got.at[1])
    tell(known.at[x], known.at[x], 2, xs)
    start1(3)
    wait(known.at[pl.ds(0, 3)], small_got.at[2])
    start1(0)

    slots = known[...].reshape(DEVICES, DEVICES)
    owner = lax.shift_right_logical(slots, 7)
    owner_t = owner.astype(jnp.float32).T.astype(jnp.bfloat16)
    down = lax.broadcasted_iota(jnp.int32, (DEVICES, DEVICES), 0)

    def entry(r, acc):
        page = table_ref[pl.ds(r, 1), :]
        high = lax.shift_right_logical(page, 7)
        low = jnp.bitwise_and(page, 127)
        pick = jnp.where(down == high, 1.0, 0.0).astype(jnp.bfloat16)
        column = jnp.dot(owner_t, pick, preferred_element_type=jnp.float32)
        mine = jnp.sum(jnp.where(down == low, column, 0.0), axis=0, keepdims=True)
        return acc + jnp.where(down == mine.astype(jnp.int32), rate_ref[r], 0.0)

    acc = lax.fori_loop(0, 16, entry, jnp.zeros((DEVICES, DEVICES), jnp.float32))
    first_sum = jnp.sum(acc.T, axis=0, keepdims=True)
    part1[...] = first_sum
    row1[pl.ds(row, 1), :] = first_sum
    to_me = jnp.where(owner == me, jnp.bitwise_and(slots, 127), 0).astype(jnp.float32)
    slot_out_ref[...] = jnp.sum(to_me.T, axis=0, keepdims=True).astype(jnp.int32)

    tell(part1, row1.at[pl.ds(row, 1)], 3, cell)
    for second in AWAY:
        for g in range(3):
            phase2((g, 0, second))
    forward2(2)
    wait(row1.at[pl.ds(0, 7)], small_got.at[3])
    second_sum = jnp.sum(row1[...], axis=0, keepdims=True)
    part2[...] = second_sum
    row2[pl.ds(z, 1), :] = second_sum
    forward2(1)
    tell(part2, row2.at[pl.ds(z, 1)], 4, zs)
    forward2(3)
    wait(row2.at[pl.ds(0, 3)], small_got.at[4])
    third_sum = jnp.sum(row2[...], axis=0, keepdims=True)
    part3[...] = third_sum
    row3[pl.ds(x, 1), :] = third_sum
    for g in range(3):
        phase3((g, 0, 0))
    for first in AWAY:
        for g in range(3):
            key = (g, first, 0)
            wait(mid1.at[span(key)], got1.at[spot(key)])
            phase3(key)
    tell(part3, row3.at[pl.ds(x, 1)], 5, xs)
    for second in AWAY:
        for g in range(3):
            key = (g, 0, second)
            wait(mid2.at[span(key)], got2.at[spot(key)])
            phase3(key)
    for second in AWAY:
        for first in AWAY:
            for g in range(3):
                key = (g, first, second)
                wait(mid2.at[span(key)], got2.at[spot(key)])
                phase3(key)
    wait(row3.at[pl.ds(0, 3)], small_got.at[5])
    load_ref[...] = jnp.sum(row3[...], axis=0, keepdims=True)

    pages = [sum(len(v) for k, v in CHUNKS.items() if k[i]) for i in (1, 2)]
    far = sum(1 for v in CHUNKS.values() for _, s, k in v if s or k)
    wait(send_ref.at[pl.ds(0, pages[0])], sent.at[0])
    wait(send_ref.at[pl.ds(0, pages[1])], sent.at[1])
    wait(send_ref.at[pl.ds(0, far)], sent.at[2])
    wait(pages_ref.at[pl.ds(0, far)], got3)
    wait(pages_ref.at[pl.ds(0, DEVICES - far)], local.at[1])
    wait(known.at[0, 0, pl.ds(0, 7)], small_sent.at[0])
    wait(known.at[0, pl.ds(0, 3)], small_sent.at[1])
    wait(known.at[pl.ds(0, 3)], small_sent.at[2])
    wait(row1.at[pl.ds(0, 7)], small_sent.at[3])
    wait(row2.at[pl.ds(0, 3)], small_sent.at[4])
    wait(row3.at[pl.ds(0, 3)], small_sent.at[5])


SMEM = pl.BlockSpec(memory_space=pltpu.SMEM)
VMEM = pl.BlockSpec(memory_space=pltpu.VMEM)
HBM = pl.BlockSpec(memory_space=pltpu.HBM)


def on_device(kv_pages, new_slot, request_rate, page_table):
    block = jax.ShapeDtypeStruct((DEVICES,) + kv_pages.shape[2:], kv_pages.dtype)
    buffer = pltpu.VMEM(block.shape, block.dtype)
    line = lambda dtype: jax.ShapeDtypeStruct((1, DEVICES), dtype)
    place = jnp.asarray(PLACE)
    packed = pl.pallas_call(
        pack_kernel,
        out_shape=block,
        in_specs=[SMEM, SMEM, HBM],
        out_specs=VMEM,
        scratch_shapes=[pltpu.SemaphoreType.DMA],
        compiler_params=pltpu.CompilerParams(vmem_limit_bytes=45 << 20),
        name="pack",
    )(new_slot, place, kv_pages)
    row = lambda n, dtype=jnp.float32: pltpu.VMEM((n, DEVICES), dtype)
    dma = pltpu.SemaphoreType.DMA
    arrived, slot, total = pl.pallas_call(
        exchange_kernel,
        out_shape=(block, line(jnp.int32), line(jnp.float32)),
        in_specs=[SMEM, VMEM, VMEM, VMEM],
        out_specs=(VMEM, VMEM, VMEM),
        scratch_shapes=[
            buffer, buffer, pltpu.VMEM((4, 4, 8, DEVICES), jnp.int32),
            row(8), row(4), row(4), row(1), row(1), row(1),
            dma((3,)), dma((48,)), dma((48,)), dma, dma((2,)), dma((6,)), dma((6,)),
        ],
        compiler_params=pltpu.CompilerParams(
            collective_id=0, has_side_effects=True, vmem_limit_bytes=20 << 20
        ),
        name="exchange",
    )(request_rate, page_table, new_slot.reshape(1, DEVICES), packed)
    migrated, load = pl.pallas_call(
        place_kernel,
        out_shape=(jax.ShapeDtypeStruct(kv_pages.shape, kv_pages.dtype), line(jnp.float32)),
        in_specs=[SMEM, SMEM, VMEM, VMEM],
        out_specs=(HBM, VMEM),
        scratch_shapes=[dma],
        compiler_params=pltpu.CompilerParams(vmem_limit_bytes=12 << 20),
        name="place",
    )(slot, place, total, arrived)
    return migrated, load.reshape(DEVICES)


def solution(mesh):
    split = Mesh(mesh.devices.reshape(4, 4, 2, mesh.shape["dev"]), AXES)
    placed = (P(AXES, None, None, None, None), P(AXES), P(AXES), P(AXES, None))
    return jax.shard_map(
        on_device,
        mesh=split,
        in_specs=placed,
        out_specs=(P(AXES, None, None, None, None), P()),
        check_vma=False,
    )
```

time: 248 us -> 115 us (0.46)
  Pallas kernels: 0 us -> 113 us
  blocking collectives: 87.5 us -> 0 us
  local copies, waits for them, and re-layouts: 53.6 us -> 1.31 us
  waiting for transfers between devices: 32.3 us -> 0 us
  starting transfers between devices: 21.8 us -> 0 us
  matrix products: 20.3 us -> 0 us
  other arithmetic: 16 us -> 0 us
  between operations: 14.8 us -> 0.67 us
    pallas_call x0 -> x3, Pallas kernels: none -> 113 us  [the longest x1 104 us: on_device(): pl.pallas_call(exchange_kernel, out_shape=(block, line(jnp.int32), line(j...]
    unnamed x2 -> x0, blocking collectives: 52.3 us -> none
    unnamed x15 -> x8, local copies, waits for them, and re-layouts: 51.5 us -> 1.31 us
    psum x4 -> x0, blocking collectives: 35.3 us -> none  [by_axis(): return functools.reduce(lax.psum, axes, value)]
    reduce_scatter x2 -> x0, waiting for transfers between devices: 32.3 us -> none  [sum_in_order(): tiles = lax.psum_scatter(tiles, axes[k], scatter_dimension=0, tiled=True)]
    all_to_all x2 -> x0, starting transfers between devices: 21.7 us -> none  [the longest x1 11.5 us: on_device(): lax.all_to_all(dest_local, NODE_DEV, split_axis=0, concat_axis=0, tiled=T...]
    dot_general x2 -> x0, matrix products: 20.3 us -> none  [the longest x1 11.3 us: on_device(): jnp.dot(place_sel, arrived.reshape(devices, -1), preferred_element_type=j...]
    scatter-add x1 -> x0, other arithmetic: 11.3 us -> none  [on_device(): jnp.zeros((devices * page_dev,), jnp.float32).at[page_table.reshape(-1)]]
  transfers between devices with their start and end apart: 4 -> 0, of which waited for: 2 -> 0; matrix products, arithmetic and copies ran while one was open for 21% -> 0% of each run, Pallas kernels for 0% -> 0%
where the time goes in v1:
time: 115 us
  Pallas kernels  113 us (98%)
  local copies, waits for them, and re-layouts  1.31 us (1%)
    pallas_call x1, Pallas kernels, on_device(): pl.pallas_call(exchange_kernel, out_shape=(block, line(jnp.int32), line(j...  104 us
    pallas_call x1, Pallas kernels, on_device(): pl.pallas_call(place_kernel, out_shape=(jax.ShapeDtypeStruct(kv_pages.sha...  4.29 us
    pallas_call x1, Pallas kernels, on_device(): pl.pallas_call(pack_kernel, out_shape=block, in_specs=[SMEM, SMEM, HBM],...  4.12 us

profile of v1, /device:TPU:1, one launch (start us, length us, event | category | flops | bytes accessed | tf_op | source)
XLA Modules:
  0.0 114.6 jit_solution(1088964846854593652)
XLA Ops:
  0.6 0.0 copy-start.1
  0.6 0.6 copy-done.1
  1.3 0.0 copy-start.2
  1.3 0.7 copy-done.2
  1.9 0.0 copy-start
  1.9 0.0 copy-start.3
  1.9 4.1 %pack.1.send_ref = bf16[128,2,16,1024]{3,2,1,0:T(8,128)(2,1)S(1)} custom-call(s32[128]{0:T(128)S(1)} %copy-done.1, s32[128]{0:T(128)S(1)} %copy-done.2, bf16[128,1,2,16,1024]{4,3,2,1,0:T(8,128)(2,1)} %pages_ref.1), custom_call_target="tpu_custom_call" | custom-call | tf_op jit(solution)/shard_map/pack/pallas_call | solution.py:251
  6.1 0.0 copy-done
  6.1 0.0 copy-done.3
  6.1 104.2 %exchange.1 = (bf16[128,2,16,1024]{3,2,1,0:T(8,128)(2,1)S(1)}, s32[1,128]{1,0:T(1,128)S(1)}, f32[1,128]{1,0:T(1,128)S(1)}) custom-call(f32[16]{0:T(128)S(1)} %copy-done.3, s32[16,128]{1,0:T(8,128)S(1)} %copy-done, s32[1,128]{1,0:T(1,128)S(1)} %bitcast.2, bf16[128,2,16,1024]{3,2,1,0:T(8,128)(2,1)S(1)} %pack.1.send_ref), custom_call_target="tpu_custom_call" | custom-call | tf_op jit(solution)/shard_map/exchange/pallas_call | solution.py:262
  110.3 4.3 %place.1 = (bf16[128,1,2,16,1024]{4,3,2,1,0:T(8,128)(2,1)}, f32[1,128]{1,0:T(1,128)}) custom-call(s32[1,128]{1,0:T(1,128)S(1)} %get-tuple-element.7.slot_ref, s32[128]{0:T(128)S(1)} %copy-done.2, f32[1,128]{1,0:T(1,128)S(1)} %get-tuple-element.8.total_ref, bf16[128,2,16,1024]{3,2,1,0:T(8,128)(2,1)S(1)} %get-tuple-element.9.pages_ref), custom_call_target="tpu_custom_call" | custom-call | tf_op jit(solution)/shard_map/place/pallas_call | solution.py:277
Async XLA Ops:
  0.6 0.7 copy-start.1
  1.3 0.7 copy-start.2
  1.9 4.1 %copy-start = (s32[16,128]{1,0:T(8,128)S(1)}, s32[16,128]{1,0:T(8,128)}, u32[]{:S(2)}) copy-start(s32[16,128]{1,0:T(8,128)} %table_ref.1) | copy-start | bytes 24580
  1.9 4.1 %copy-start.3 = (f32[16]{0:T(128)S(1)}, f32[16]{0:T(128)}, u32[]{:S(2)}) copy-start(f32[16]{0:T(128)} %rate_ref.1) | copy-start | bytes 196

commit v2 on v1

--- a/solution.py
+++ b/solution.py
@@ -13,6 +13,7 @@
 ORDERS = (("x", "y", "z"), ("y", "z", "x"), ("z", "x", "y"))
 LATE = (2, 1, 3, 0)
 AWAY = (2, 1, 3)
+LATE_SUM = 3
 
 
 def make_plan():
@@ -28,10 +29,10 @@
     for row, (group, first, second, third, core, rel) in enumerate(keyed):
         place[rel] = row
         chunks.setdefault((group, first, second), []).append((row, third, core))
-    return place, chunks
-
-
-PLACE, CHUNKS = make_plan()
+    return place, chunks, [k[-1] for k in keyed]
+
+
+PLACE, CHUNKS, STEPS = make_plan()
 
 
 def my_index():
@@ -50,19 +51,10 @@
     return partner(**{axis: step, "c": core})
 
 
-def pack_kernel(slot_ref, place_ref, pages_ref, out_ref, sem):
+def place_kernel(slot_ref, total_ref, pages_ref, out_ref, load_ref, place_ref, sem):
     me = my_index()
-
-    @pl.loop(0, DEVICES)
-    def _(p):
-        row = place_ref[jnp.bitwise_xor(lax.shift_right_logical(slot_ref[p], 7), me)]
-        pltpu.make_async_copy(pages_ref.at[p, 0], out_ref.at[row], sem).start()
-
-    pltpu.make_async_copy(out_ref, out_ref, sem).wait()
-
-
-def place_kernel(slot_ref, place_ref, total_ref, pages_ref, out_ref, load_ref, sem):
-    me = my_index()
+    for rel in range(DEVICES):
+        place_ref[rel] = int(PLACE[rel])
 
     @pl.loop(0, DEVICES)
     def _(e):
@@ -74,9 +66,9 @@
 
 
 def exchange_kernel(
-    rate_ref, table_ref, slots_ref, send_ref,
+    rate_in, table_in, slots_in, stored_ref,
     pages_ref, slot_out_ref, load_ref,
-    mid1, mid2, known, row1, row2, row3, part1, part2, part3,
+    rate_ref, table_ref, slots_ref, stay, send_ref, mid1, mid2, index_row, index, known, row1, row2, row3, part1, part2, part3,
     sent, got1, got2, got3, local, small_sent, small_got,
 ):
     x, z, c, y = (lax.axis_index(a) for a in AXES)
@@ -89,13 +81,36 @@
     def wait(ref, sem):
         pltpu.make_async_copy(ref, ref, sem).wait()
 
-    keep = pltpu.make_async_copy(slots_ref, known.at[x, z, pl.ds(row, 1)], local.at[0])
-    keep.start()
+    small = [
+        pltpu.make_async_copy(src, dst, local.at[4 + k])
+        for k, (src, dst) in enumerate(
+            ((slots_in, slots_ref), (table_in, table_ref), (rate_in, rate_ref))
+        )
+    ]
+    load = pltpu.make_async_copy(stored_ref.at[:, 0], stay, local.at[2])
+    keep = pltpu.make_async_copy(slots_in, known.at[x, z, pl.ds(row, 1)], local.at[0])
+    small[0].start()
+    load.start()
     barrier = pltpu.get_barrier_semaphore()
     peers = [partner(c=1)] + [along(a, s, k) for a in "xyz" for s in AWAY for k in (0, 1)]
     for dev in peers:
         pl.semaphore_signal(barrier, inc=1, device_id=dev, device_id_type=pl.DeviceIdType.MESH)
+    keep.start()
+    small[1].start()
+    small[2].start()
+    small[0].wait()
+    down = lax.broadcasted_iota(jnp.int32, (DEVICES, DEVICES), 0)
+    right = lax.broadcasted_iota(jnp.int32, (DEVICES, DEVICES), 1)
+    step_row = jnp.bitwise_xor(lax.shift_right_logical(slots_ref[...], 7), me)
+    found = jnp.where(down == step_row, right, 0).astype(jnp.float32)
+    index_row[...] = jnp.bitwise_and(
+        jnp.sum(found.T, axis=0, keepdims=True).astype(jnp.int32), DEVICES - 1
+    )
     pl.semaphore_wait(barrier, len(peers))
+    fetch = pltpu.make_async_copy(index_row, index, local.at[3])
+    fetch.start()
+    fetch.wait()
+    load.wait()
 
     cell = [partner(c=k, y=s) for k in (0, 1) for s in range(4) if k or s]
 
@@ -145,6 +160,17 @@
                 wait(mid1.at[span(key)], got1.at[spot(key)])
                 phase2(key)
 
+    def pack(keys):
+        for key in keys:
+            for page, _, _ in CHUNKS[key]:
+                send_ref[page] = stay[index[0, STEPS[page]]]
+
+    def block(second):
+        return [(g, first, second) for first in AWAY for g in range(3)]
+
+    def near(seconds):
+        return [(g, 0, second) for second in seconds for g in range(3)]
+
     def tell(src, dst, k, devs):
         for dev in devs:
             remote(src, dst, small_sent.at[k], small_got.at[k], dev).start()
@@ -152,22 +178,33 @@
     zs = [partner(z=s) for s in AWAY]
     xs = [partner(x=s) for s in AWAY]
 
+    pack(block(2))
     tell(slots_ref, known.at[x, z, pl.ds(row, 1)], 0, cell)
+    pack(block(1)[:3])
     start1(2)
+    pack(block(1)[3:])
+    pack(block(3))
+    start1(1)
+    pack(block(0))
     keep.wait()
     wait(known.at[0, 0, pl.ds(0, 7)], small_got.at[0])
     tell(known.at[x, z], known.at[x, z], 1, zs)
-    start1(1)
+    start1(3)
     wait(known.at[0, pl.ds(0, 3)], small_got.at[1])
     tell(known.at[x], known.at[x], 2, xs)
-    start1(3)
+    pack(near(AWAY))
+    start1(0)
+    pack(near((0,)))
+    for second in AWAY:
+        for g in range(3):
+            phase2((g, 0, second))
     wait(known.at[pl.ds(0, 3)], small_got.at[2])
-    start1(0)
-
+
+    small[1].wait()
+    small[2].wait()
     slots = known[...].reshape(DEVICES, DEVICES)
     owner = lax.shift_right_logical(slots, 7)
     owner_t = owner.astype(jnp.float32).T.astype(jnp.bfloat16)
-    down = lax.broadcasted_iota(jnp.int32, (DEVICES, DEVICES), 0)
 
     def entry(r, acc):
         page = table_ref[pl.ds(r, 1), :]
@@ -187,39 +224,37 @@
 
     tell(part1, row1.at[pl.ds(row, 1)], 3, cell)
     for second in AWAY:
-        for g in range(3):
-            phase2((g, 0, second))
-    forward2(2)
+        forward2(second)
     wait(row1.at[pl.ds(0, 7)], small_got.at[3])
     second_sum = jnp.sum(row1[...], axis=0, keepdims=True)
     part2[...] = second_sum
     row2[pl.ds(z, 1), :] = second_sum
-    forward2(1)
-    tell(part2, row2.at[pl.ds(z, 1)], 4, zs)
-    forward2(3)
-    wait(row2.at[pl.ds(0, 3)], small_got.at[4])
-    third_sum = jnp.sum(row2[...], axis=0, keepdims=True)
-    part3[...] = third_sum
-    row3[pl.ds(x, 1), :] = third_sum
     for g in range(3):
         phase3((g, 0, 0))
+    tell(part2, row2.at[pl.ds(z, 1)], 4, zs)
     for first in AWAY:
         for g in range(3):
             key = (g, first, 0)
             wait(mid1.at[span(key)], got1.at[spot(key)])
             phase3(key)
-    tell(part3, row3.at[pl.ds(x, 1)], 5, xs)
     for second in AWAY:
         for g in range(3):
             key = (g, 0, second)
             wait(mid2.at[span(key)], got2.at[spot(key)])
             phase3(key)
     for second in AWAY:
+        if second == LATE_SUM:
+            wait(row2.at[pl.ds(0, 3)], small_got.at[4])
+            third_sum = jnp.sum(row2[...], axis=0, keepdims=True)
+            part3[...] = third_sum
+            row3[pl.ds(x, 1), :] = third_sum
         for first in AWAY:
             for g in range(3):
                 key = (g, first, second)
                 wait(mid2.at[span(key)], got2.at[spot(key)])
                 phase3(key)
+            if second == LATE_SUM and first == 2:
+                tell(part3, row3.at[pl.ds(x, 1)], 5, xs)
     wait(row3.at[pl.ds(0, 3)], small_got.at[5])
     load_ref[...] = jnp.sum(row3[...], axis=0, keepdims=True)
 
@@ -247,42 +282,35 @@
     block = jax.ShapeDtypeStruct((DEVICES,) + kv_pages.shape[2:], kv_pages.dtype)
     buffer = pltpu.VMEM(block.shape, block.dtype)
     line = lambda dtype: jax.ShapeDtypeStruct((1, DEVICES), dtype)
-    place = jnp.asarray(PLACE)
-    packed = pl.pallas_call(
-        pack_kernel,
-        out_shape=block,
-        in_specs=[SMEM, SMEM, HBM],
-        out_specs=VMEM,
-        scratch_shapes=[pltpu.SemaphoreType.DMA],
-        compiler_params=pltpu.CompilerParams(vmem_limit_bytes=45 << 20),
-        name="pack",
-    )(new_slot, place, kv_pages)
     row = lambda n, dtype=jnp.float32: pltpu.VMEM((n, DEVICES), dtype)
     dma = pltpu.SemaphoreType.DMA
     arrived, slot, total = pl.pallas_call(
         exchange_kernel,
         out_shape=(block, line(jnp.int32), line(jnp.float32)),
-        in_specs=[SMEM, VMEM, VMEM, VMEM],
+        in_specs=[HBM] * 4,
         out_specs=(VMEM, VMEM, VMEM),
         scratch_shapes=[
-            buffer, buffer, pltpu.VMEM((4, 4, 8, DEVICES), jnp.int32),
+            pltpu.SMEM((16,), jnp.float32), row(16, jnp.int32), row(1, jnp.int32),
+            buffer, buffer, buffer, buffer, row(1, jnp.int32), pltpu.SMEM((1, DEVICES), jnp.int32),
+            pltpu.VMEM((4, 4, 8, DEVICES), jnp.int32),
             row(8), row(4), row(4), row(1), row(1), row(1),
-            dma((3,)), dma((48,)), dma((48,)), dma, dma((2,)), dma((6,)), dma((6,)),
+            dma((3,)), dma((48,)), dma((48,)), dma, dma((7,)), dma((6,)), dma((6,)),
         ],
         compiler_params=pltpu.CompilerParams(
-            collective_id=0, has_side_effects=True, vmem_limit_bytes=20 << 20
+            collective_id=0, has_side_effects=True, vmem_limit_bytes=36 << 20
         ),
         name="exchange",
-    )(request_rate, page_table, new_slot.reshape(1, DEVICES), packed)
+    )(*(pltpu.with_memory_space_constraint(v, pltpu.HBM)
+        for v in (request_rate, page_table, new_slot.reshape(1, DEVICES), kv_pages)))
     migrated, load = pl.pallas_call(
         place_kernel,
         out_shape=(jax.ShapeDtypeStruct(kv_pages.shape, kv_pages.dtype), line(jnp.float32)),
-        in_specs=[SMEM, SMEM, VMEM, VMEM],
+        in_specs=[SMEM, VMEM, VMEM],
         out_specs=(HBM, VMEM),
-        scratch_shapes=[dma],
+        scratch_shapes=[pltpu.SMEM((DEVICES,), jnp.int32), dma],
         compiler_params=pltpu.CompilerParams(vmem_limit_bytes=12 << 20),
         name="place",
-    )(slot, place, total, arrived)
+    )(slot, total, arrived)
     return migrated, load.reshape(DEVICES)
 
 

time: 115 us -> 108 us (0.939)
  Pallas kernels: 113 us -> 107 us
  local copies, waits for them, and re-layouts: 1.31 us -> 0 us
    pallas_call x1 -> x0, Pallas kernels: 4.12 us -> none  [on_device(): pl.pallas_call(pack_kernel, out_shape=block, in_specs=[SMEM, SMEM, HBM],...]
    pallas_call x1, Pallas kernels: 104 us -> 103 us  [on_device(): pl.pallas_call(exchange_kernel, out_shape=(block, line(jnp.int32), line(j...]
    unnamed x8 -> x0, local copies, waits for them, and re-layouts: 1.31 us -> none
where the time goes in v2:
time: 108 us
  Pallas kernels  107 us (99%)
    pallas_call x1, Pallas kernels, on_device(): pl.pallas_call(exchange_kernel, out_shape=(block, line(jnp.int32), line(j...  103 us
    pallas_call x1, Pallas kernels, on_device(): pl.pallas_call(place_kernel, out_shape=(jax.ShapeDtypeStruct(kv_pages.sha...  4.35 us

profile of v2, /device:TPU:1, one launch (start us, length us, event | category | flops | bytes accessed | tf_op | source)
XLA Modules:
  0.0 107.6 jit_solution(10179495953634296491)
XLA Ops:
  0.6 102.6 %exchange.1 = (bf16[128,2,16,1024]{3,2,1,0:T(8,128)(2,1)S(1)}, s32[1,128]{1,0:T(1,128)S(1)}, f32[1,128]{1,0:T(1,128)S(1)}) custom-call(f32[16]{0:T(128)} %rate_in.1, s32[16,128]{1,0:T(8,128)} %table_in.1, s32[1,128]{1,0:T(1,128)} %bitcast.2, bf16[128,1,2,16,1024]{4,3,2,1,0:T(8,128)(2,1)} %stored_ref.1), custom_call_target="tpu_custom_call" | custom-call | tf_op jit(solution)/shard_map/exchange/pallas_call | solution.py:287
  103.3 4.3 %place.1 = (bf16[128,1,2,16,1024]{4,3,2,1,0:T(8,128)(2,1)}, f32[1,128]{1,0:T(1,128)}) custom-call(s32[1,128]{1,0:T(1,128)S(1)} %get-tuple-element.7.slot_ref, f32[1,128]{1,0:T(1,128)S(1)} %get-tuple-element.8.total_ref, bf16[128,2,16,1024]{3,2,1,0:T(8,128)(2,1)S(1)} %get-tuple-element.9.pages_ref), custom_call_target="tpu_custom_call" | custom-call | tf_op jit(solution)/shard_map/place/pallas_call | solution.py:305

commit v3 on v2

--- a/solution.py
+++ b/solution.py
@@ -40,6 +40,13 @@
     return ((at[0] * 4 + at[1]) * 2 + at[2]) * 4 + at[3]
 
 
+def core_first(index):
+    return (
+        (index & 4) * 16 + (lax.shift_right_logical(index, 5)) * 16
+        + (lax.shift_right_logical(index, 1) & 12) + (index & 3)
+    )
+
+
 def partner(**steps):
     return tuple(
         jnp.bitwise_xor(lax.axis_index(a), steps[a]) if steps.get(a) else lax.axis_index(a)
@@ -52,9 +59,10 @@
 
 
 def place_kernel(slot_ref, total_ref, pages_ref, out_ref, load_ref, place_ref, sem):
-    me = my_index()
+    me = core_first(my_index())
     for rel in range(DEVICES):
-        place_ref[rel] = int(PLACE[rel])
+        at = (rel & 4) * 16 + (rel >> 5) * 16 + (rel >> 1 & 12) + (rel & 3)
+        place_ref[at] = int(PLACE[rel])
 
     @pl.loop(0, DEVICES)
     def _(e):
@@ -68,12 +76,12 @@
 def exchange_kernel(
     rate_in, table_in, slots_in, stored_ref,
     pages_ref, slot_out_ref, load_ref,
-    rate_ref, table_ref, slots_ref, stay, send_ref, mid1, mid2, index_row, index, known, row1, row2, row3, part1, part2, part3,
+    rate_ref, table_ref, slots_ref, stay, send_ref, mid1, mid2, index_row, index, known, row0, row1, row2, row3, part0, part1, part2, part3,
     sent, got1, got2, got3, local, small_sent, small_got,
 ):
     x, z, c, y = (lax.axis_index(a) for a in AXES)
     me = my_index()
-    row = c * 4 + y
+    row = z * 4 + y
     remote = lambda src, dst, ss, rs, dev: pltpu.make_async_remote_copy(
         src, dst, ss, rs, device_id=dev, device_id_type=pl.DeviceIdType.MESH
     )
@@ -88,7 +96,7 @@
         )
     ]
     load = pltpu.make_async_copy(stored_ref.at[:, 0], stay, local.at[2])
-    keep = pltpu.make_async_copy(slots_in, known.at[x, z, pl.ds(row, 1)], local.at[0])
+    keep = pltpu.make_async_copy(slots_in, known.at[c, x, pl.ds(row, 1)], local.at[0])
     small[0].start()
     load.start()
     barrier = pltpu.get_barrier_semaphore()
@@ -106,13 +114,13 @@
     index_row[...] = jnp.bitwise_and(
         jnp.sum(found.T, axis=0, keepdims=True).astype(jnp.int32), DEVICES - 1
     )
-    pl.semaphore_wait(barrier, len(peers))
     fetch = pltpu.make_async_copy(index_row, index, local.at[3])
     fetch.start()
     fetch.wait()
     load.wait()
 
-    cell = [partner(c=k, y=s) for k in (0, 1) for s in range(4) if k or s]
+    twin = [partner(c=1)]
+    ys = [partner(y=s) for s in AWAY]
 
     def span(key):
         rows = CHUNKS[key]
@@ -139,7 +147,7 @@
 
     def phase3(key):
         src = source(key)
-        for page, step, core in CHUNKS[key]:
+        for page, step, core in sorted(CHUNKS[key], key=lambda v: v[1] != 2):
             if step or core:
                 remote(
                     src.at[page], pages_ref.at[page], sent.at[2], got3,
@@ -178,27 +186,34 @@
     zs = [partner(z=s) for s in AWAY]
     xs = [partner(x=s) for s in AWAY]
 
-    pack(block(2))
-    tell(slots_ref, known.at[x, z, pl.ds(row, 1)], 0, cell)
-    pack(block(1)[:3])
-    start1(2)
-    pack(block(1)[3:])
+    front = block(2) + block(1)
+    pack(front[:6])
+    pl.semaphore_wait(barrier, len(peers))
+    for at in (0, 3, 6):
+        for key in front[at : at + 3]:
+            phase1(key)
+        pack(front[at + 6 : at + 9])
+    tell(slots_ref, known.at[c, x, pl.ds(row, 1)], 0, ys)
+    pack(front[15:])
+    for key in front[9:]:
+        phase1(key)
     pack(block(3))
-    start1(1)
     pack(block(0))
     keep.wait()
-    wait(known.at[0, 0, pl.ds(0, 7)], small_got.at[0])
-    tell(known.at[x, z], known.at[x, z], 1, zs)
+    wait(known.at[0, 0, pl.ds(0, 3)], small_got.at[0])
+    tell(known.at[c, x, pl.ds(z * 4, 4)], known.at[c, x, pl.ds(z * 4, 4)], 1, zs)
     start1(3)
-    wait(known.at[0, pl.ds(0, 3)], small_got.at[1])
-    tell(known.at[x], known.at[x], 2, xs)
     pack(near(AWAY))
+    wait(known.at[0, 0, pl.ds(0, 12)], small_got.at[1])
+    tell(known.at[c, x], known.at[c, x], 2, xs)
     start1(0)
     pack(near((0,)))
     for second in AWAY:
         for g in range(3):
             phase2((g, 0, second))
-    wait(known.at[pl.ds(0, 3)], small_got.at[2])
+    wait(known.at[0, pl.ds(0, 3)], small_got.at[2])
+    tell(known.at[c], known.at[c], 6, twin)
+    wait(known.at[0], small_got.at[6])
 
     small[1].wait()
     small[2].wait()
@@ -208,7 +223,7 @@
 
     def entry(r, acc):
         page = table_ref[pl.ds(r, 1), :]
-        high = lax.shift_right_logical(page, 7)
+        high = core_first(lax.shift_right_logical(page, 7))
         low = jnp.bitwise_and(page, 127)
         pick = jnp.where(down == high, 1.0, 0.0).astype(jnp.bfloat16)
         column = jnp.dot(owner_t, pick, preferred_element_type=jnp.float32)
@@ -217,15 +232,20 @@
 
     acc = lax.fori_loop(0, 16, entry, jnp.zeros((DEVICES, DEVICES), jnp.float32))
     first_sum = jnp.sum(acc.T, axis=0, keepdims=True)
-    part1[...] = first_sum
-    row1[pl.ds(row, 1), :] = first_sum
+    part0[...] = first_sum
     to_me = jnp.where(owner == me, jnp.bitwise_and(slots, 127), 0).astype(jnp.float32)
     slot_out_ref[...] = jnp.sum(to_me.T, axis=0, keepdims=True).astype(jnp.int32)
 
-    tell(part1, row1.at[pl.ds(row, 1)], 3, cell)
-    for second in AWAY:
+    tell(part0, row0, 7, twin)
+    wait(row0, small_got.at[7])
+    first_sum = part0[...] + row0[...]
+    part1[...] = first_sum
+    row1[pl.ds(y, 1), :] = first_sum
+    forward2(AWAY[0])
+    tell(part1, row1.at[pl.ds(y, 1)], 3, ys)
+    for second in AWAY[1:]:
         forward2(second)
-    wait(row1.at[pl.ds(0, 7)], small_got.at[3])
+    wait(row1.at[pl.ds(0, 3)], small_got.at[3])
     second_sum = jnp.sum(row1[...], axis=0, keepdims=True)
     part2[...] = second_sum
     row2[pl.ds(z, 1), :] = second_sum
@@ -265,10 +285,12 @@
     wait(send_ref.at[pl.ds(0, far)], sent.at[2])
     wait(pages_ref.at[pl.ds(0, far)], got3)
     wait(pages_ref.at[pl.ds(0, DEVICES - far)], local.at[1])
-    wait(known.at[0, 0, pl.ds(0, 7)], small_sent.at[0])
-    wait(known.at[0, pl.ds(0, 3)], small_sent.at[1])
-    wait(known.at[pl.ds(0, 3)], small_sent.at[2])
-    wait(row1.at[pl.ds(0, 7)], small_sent.at[3])
+    wait(known.at[0, 0, pl.ds(0, 3)], small_sent.at[0])
+    wait(known.at[0, 0, pl.ds(0, 12)], small_sent.at[1])
+    wait(known.at[0, pl.ds(0, 3)], small_sent.at[2])
+    wait(known.at[0], small_sent.at[6])
+    wait(row0, small_sent.at[7])
+    wait(row1.at[pl.ds(0, 3)], small_sent.at[3])
     wait(row2.at[pl.ds(0, 3)], small_sent.at[4])
     wait(row3.at[pl.ds(0, 3)], small_sent.at[5])
 
@@ -292,9 +314,9 @@
         scratch_shapes=[
             pltpu.SMEM((16,), jnp.float32), row(16, jnp.int32), row(1, jnp.int32),
             buffer, buffer, buffer, buffer, row(1, jnp.int32), pltpu.SMEM((1, DEVICES), jnp.int32),
-            pltpu.VMEM((4, 4, 8, DEVICES), jnp.int32),
-            row(8), row(4), row(4), row(1), row(1), row(1),
-            dma((3,)), dma((48,)), dma((48,)), dma, dma((7,)), dma((6,)), dma((6,)),
+            pltpu.VMEM((2, 4, 16, DEVICES), jnp.int32),
+            row(1), row(4), row(4), row(4), row(1), row(1), row(1), row(1),
+            dma((3,)), dma((48,)), dma((48,)), dma, dma((7,)), dma((8,)), dma((8,)),
         ],
         compiler_params=pltpu.CompilerParams(
             collective_id=0, has_side_effects=True, vmem_limit_bytes=36 << 20

time: 108 us -> 106 us (0.981)
    pallas_call x1, Pallas kernels: 103 us -> 101 us  [on_device(): pl.pallas_call(exchange_kernel, out_shape=(block, line(jnp.int32), line(j...]
where the time goes in v3:
time: 106 us
  Pallas kernels  106 us (100%)
    pallas_call x1, Pallas kernels, on_device(): pl.pallas_call(exchange_kernel, out_shape=(block, line(jnp.int32), line(j...  101 us
    pallas_call x1, Pallas kernels, on_device(): pl.pallas_call(place_kernel, out_shape=(jax.ShapeDtypeStruct(kv_pages.sha...  4.35 us

profile of v3, /device:TPU:1, one launch (start us, length us, event | category | flops | bytes accessed | tf_op | source)
XLA Modules:
  0.0 106.3 jit_solution(12911737122710242064)
XLA Ops:
  0.6 101.3 %exchange.1 = (bf16[128,2,16,1024]{3,2,1,0:T(8,128)(2,1)S(1)}, s32[1,128]{1,0:T(1,128)S(1)}, f32[1,128]{1,0:T(1,128)S(1)}) custom-call(f32[16]{0:T(128)} %rate_in.1, s32[16,128]{1,0:T(8,128)} %table_in.1, s32[1,128]{1,0:T(1,128)} %bitcast.2, bf16[128,1,2,16,1024]{4,3,2,1,0:T(8,128)(2,1)} %stored_ref.1), custom_call_target="tpu_custom_call" | custom-call | tf_op jit(solution)/shard_map/exchange/pallas_call | solution.py:309
  101.9 4.3 %place.1 = (bf16[128,1,2,16,1024]{4,3,2,1,0:T(8,128)(2,1)}, f32[1,128]{1,0:T(1,128)}) custom-call(s32[1,128]{1,0:T(1,128)S(1)} %get-tuple-element.7.slot_ref, f32[1,128]{1,0:T(1,128)S(1)} %get-tuple-element.8.total_ref, bf16[128,2,16,1024]{3,2,1,0:T(8,128)(2,1)S(1)} %get-tuple-element.9.pages_ref), custom_call_target="tpu_custom_call" | custom-call | tf_op jit(solution)/shard_map/place/pallas_call | solution.py:327

commit v4 on v3

--- a/solution.py
+++ b/solution.py
@@ -58,19 +58,24 @@
     return partner(**{axis: step, "c": core})
 
 
-def place_kernel(slot_ref, total_ref, pages_ref, out_ref, load_ref, place_ref, sem):
+def place_kernel(slot_in, total_ref, pages_ref, out_ref, load_ref, slot_ref, place_ref, sems):
+    fetch = pltpu.make_async_copy(slot_in, slot_ref, sems.at[0])
+    fetch.start()
+    load = pltpu.make_async_copy(total_ref, load_ref, sems.at[1])
+    load.start()
     me = core_first(my_index())
     for rel in range(DEVICES):
         at = (rel & 4) * 16 + (rel >> 5) * 16 + (rel >> 1 & 12) + (rel & 3)
         place_ref[at] = int(PLACE[rel])
+    fetch.wait()
 
     @pl.loop(0, DEVICES)
     def _(e):
         row = place_ref[jnp.bitwise_xor(e, me)]
-        pltpu.make_async_copy(pages_ref.at[row], out_ref.at[slot_ref[0, e], 0], sem).start()
-
-    load_ref[...] = total_ref[...] * (1.0 / 2048.0)
-    pltpu.make_async_copy(pages_ref, pages_ref, sem).wait()
+        pltpu.make_async_copy(pages_ref.at[row], out_ref.at[slot_ref[0, e], 0], sems.at[2]).start()
+
+    load.wait()
+    pltpu.make_async_copy(pages_ref, pages_ref, sems.at[2]).wait()
 
 
 def exchange_kernel(
@@ -192,20 +197,21 @@
     for at in (0, 3, 6):
         for key in front[at : at + 3]:
             phase1(key)
+        if at == 0:
+            tell(slots_ref, known.at[c, x, pl.ds(row, 1)], 0, ys)
         pack(front[at + 6 : at + 9])
-    tell(slots_ref, known.at[c, x, pl.ds(row, 1)], 0, ys)
+    keep.wait()
+    wait(known.at[0, 0, pl.ds(0, 3)], small_got.at[0])
+    tell(known.at[c, x, pl.ds(z * 4, 4)], known.at[c, x, pl.ds(z * 4, 4)], 1, zs)
     pack(front[15:])
     for key in front[9:]:
         phase1(key)
     pack(block(3))
     pack(block(0))
-    keep.wait()
-    wait(known.at[0, 0, pl.ds(0, 3)], small_got.at[0])
-    tell(known.at[c, x, pl.ds(z * 4, 4)], known.at[c, x, pl.ds(z * 4, 4)], 1, zs)
+    wait(known.at[0, 0, pl.ds(0, 12)], small_got.at[1])
+    tell(known.at[c, x], known.at[c, x], 2, xs)
     start1(3)
     pack(near(AWAY))
-    wait(known.at[0, 0, pl.ds(0, 12)], small_got.at[1])
-    tell(known.at[c, x], known.at[c, x], 2, xs)
     start1(0)
     pack(near((0,)))
     for second in AWAY:
@@ -276,7 +282,7 @@
             if second == LATE_SUM and first == 2:
                 tell(part3, row3.at[pl.ds(x, 1)], 5, xs)
     wait(row3.at[pl.ds(0, 3)], small_got.at[5])
-    load_ref[...] = jnp.sum(row3[...], axis=0, keepdims=True)
+    load_ref[...] = jnp.sum(row3[...], axis=0, keepdims=True) * (1.0 / 2048.0)
 
     pages = [sum(len(v) for k, v in CHUNKS.items() if k[i]) for i in (1, 2)]
     far = sum(1 for v in CHUNKS.values() for _, s, k in v if s or k)
@@ -327,9 +333,11 @@
     migrated, load = pl.pallas_call(
         place_kernel,
         out_shape=(jax.ShapeDtypeStruct(kv_pages.shape, kv_pages.dtype), line(jnp.float32)),
-        in_specs=[SMEM, VMEM, VMEM],
-        out_specs=(HBM, VMEM),
-        scratch_shapes=[pltpu.SMEM((DEVICES,), jnp.int32), dma],
+        in_specs=[VMEM, VMEM, VMEM],
+        out_specs=(HBM, HBM),
+        scratch_shapes=[
+            pltpu.SMEM((1, DEVICES), jnp.int32), pltpu.SMEM((DEVICES,), jnp.int32), dma((3,)),
+        ],
         compiler_params=pltpu.CompilerParams(vmem_limit_bytes=12 << 20),
         name="place",
     )(slot, total, arrived)

time: 106 us -> 106 us (level)
  no operation moved by 1% of the time
where the time goes in v4:
time: 106 us; the launch traced here: 105 us
  Pallas kernels  105 us (99%)
    pallas_call x1, Pallas kernels, on_device(): pl.pallas_call(exchange_kernel, out_shape=(block, line(jnp.int32), line(j...  101 us
    pallas_call x1, Pallas kernels, on_device(): pl.pallas_call(place_kernel, out_shape=(jax.ShapeDtypeStruct(kv_pages.sha...  3.78 us

profile of v4, /device:TPU:1, one launch (start us, length us, event | category | flops | bytes accessed | tf_op | source)
XLA Modules:
  0.0 105.5 jit_solution(8813002972900371974)
XLA Ops:
  0.6 101.1 %exchange.1 = (bf16[128,2,16,1024]{3,2,1,0:T(8,128)(2,1)S(1)}, s32[1,128]{1,0:T(1,128)S(1)}, f32[1,128]{1,0:T(1,128)S(1)}) custom-call(f32[16]{0:T(128)} %rate_in.1, s32[16,128]{1,0:T(8,128)} %table_in.1, s32[1,128]{1,0:T(1,128)} %bitcast.2, bf16[128,1,2,16,1024]{4,3,2,1,0:T(8,128)(2,1)} %stored_ref.1), custom_call_target="tpu_custom_call" | custom-call | tf_op jit(solution)/shard_map/exchange/pallas_call | solution.py:315
  101.7 3.8 %place.1 = (bf16[128,1,2,16,1024]{4,3,2,1,0:T(8,128)(2,1)}, f32[1,128]{1,0:T(1,128)}) custom-call(s32[1,128]{1,0:T(1,128)S(1)} %get-tuple-element.7.slot_in, f32[1,128]{1,0:T(1,128)S(1)} %get-tuple-element.8.total_ref, bf16[128,2,16,1024]{3,2,1,0:T(8,128)(2,1)S(1)} %get-tuple-element.9.pages_ref), custom_call_target="tpu_custom_call" | custom-call | tf_op jit(solution)/shard_map/place/pallas_call | solution.py:333

commit v5 on v4

--- a/solution.py
+++ b/solution.py
@@ -105,7 +105,7 @@
     small[0].start()
     load.start()
     barrier = pltpu.get_barrier_semaphore()
-    peers = [partner(c=1)] + [along(a, s, k) for a in "xyz" for s in AWAY for k in (0, 1)]
+    peers = [partner(c=1)] + [along(a, s) for a in "xyz" for s in AWAY]
     for dev in peers:
         pl.semaphore_signal(barrier, inc=1, device_id=dev, device_id_type=pl.DeviceIdType.MESH)
     keep.start()
@@ -206,13 +206,13 @@
     pack(front[15:])
     for key in front[9:]:
         phase1(key)
+    pack(block(0))
     pack(block(3))
-    pack(block(0))
     wait(known.at[0, 0, pl.ds(0, 12)], small_got.at[1])
     tell(known.at[c, x], known.at[c, x], 2, xs)
+    start1(0)
+    pack(near(AWAY))
     start1(3)
-    pack(near(AWAY))
-    start1(0)
     pack(near((0,)))
     for second in AWAY:
         for g in range(3):

time: 106 us -> 105 us (level)
  no operation moved by 1% of the time
where the time goes in v5:
time: 105 us
  Pallas kernels  104 us (99%)
    pallas_call x1, Pallas kernels, on_device(): pl.pallas_call(exchange_kernel, out_shape=(block, line(jnp.int32), line(j...  101 us
    pallas_call x1, Pallas kernels, on_device(): pl.pallas_call(place_kernel, out_shape=(jax.ShapeDtypeStruct(kv_pages.sha...  3.78 us

profile of v5, /device:TPU:1, one launch (start us, length us, event | category | flops | bytes accessed | tf_op | source)
XLA Modules:
  0.0 105.0 jit_solution(5028093801476287319)
XLA Ops:
  0.6 100.6 %exchange.1 = (bf16[128,2,16,1024]{3,2,1,0:T(8,128)(2,1)S(1)}, s32[1,128]{1,0:T(1,128)S(1)}, f32[1,128]{1,0:T(1,128)S(1)}) custom-call(f32[16]{0:T(128)} %rate_in.1, s32[16,128]{1,0:T(8,128)} %table_in.1, s32[1,128]{1,0:T(1,128)} %bitcast.2, bf16[128,1,2,16,1024]{4,3,2,1,0:T(8,128)(2,1)} %stored_ref.1), custom_call_target="tpu_custom_call" | custom-call | tf_op jit(solution)/shard_map/exchange/pallas_call | solution.py:315
  101.2 3.8 %place.1 = (bf16[128,1,2,16,1024]{4,3,2,1,0:T(8,128)(2,1)}, f32[1,128]{1,0:T(1,128)}) custom-call(s32[1,128]{1,0:T(1,128)S(1)} %get-tuple-element.7.slot_in, f32[1,128]{1,0:T(1,128)S(1)} %get-tuple-element.8.total_ref, bf16[128,2,16,1024]{3,2,1,0:T(8,128)(2,1)S(1)} %get-tuple-element.9.pages_ref), custom_call_target="tpu_custom_call" | custom-call | tf_op jit(solution)/shard_map/place/pallas_call | solution.py:333
